TPU v7x, 256 devices: a whole 4x4x8 slice. The times are simulated.
256 devices in a mesh: dp: 256 (over z, x, y, core).
Axes of the slice: x: 4, y: 4, z: 8, core: 2. Of those that a mesh axis runs over, the one named last changes fastest.
Arguments:
- images: bfloat16 [1024, 92, 4096], P('dp'), may hold values from -6 to 6
- layer_gain: float32 [4096], replicated, may hold values from 0.5 to 1.5
- in_weight: bfloat16 [4096, 1024], replicated, may hold values from -1 to 1
- out_weight: bfloat16 [1024, 1024], replicated, may hold values from -1 to 1
- text_embed: bfloat16 [1024, 1024], P('dp'), may hold values from -6 to 6
- pair_index: int32 [1024], P('dp'), may hold values from 0 to 1023, each once
- logit_scale: float32 [1], replicated, may hold values from 30 to 200
Outputs:
- loss: float32 [1], replicated
- grad_norm: float32 [1], replicated
- update_image: float32 [1024, 1024], P('dp')
- update_text: float32 [1024, 1024], P('dp')
Inputs may be any that keep to these rules, and one draw needn't show every extreme that they name: Image i is paired with text row pair_index[i]; every text row is paired with exactly one image.
All inputs are finite; a program needn't handle non-finite values.
Results may differ from a plain program's by a relative error of at most 0.0086.
Values may be sent and summed in bfloat16 or wider, within the bound.
A program may use at most 64 MiB of HBM per device.

v0:
```python
import jax
import jax.numpy as jnp
from jax import lax
from jax.sharding import Mesh
from jax.sharding import PartitionSpec as P

DP = ("dp_0", "dp_1", "dp_2", "dp_3")
EPS_UNIT = 1e-06
EPS_LAYER = 1e-05


def from_everyone(array, axis):
    size = lax.axis_size(axis)
    return lax.all_to_all(
        jnp.broadcast_to(array[None], (size, *array.shape)), axis, 0, 0, tiled=True
    )


def laid_out(blocks, dim):
    lengths = list(blocks.shape[1:])
    lengths[dim] *= blocks.shape[0]
    return jnp.moveaxis(blocks, 0, dim).reshape(lengths)


def whole_of(array, axes, dim):
    far, near = axes
    first = from_everyone(array, far)
    blocks = jnp.swapaxes(from_everyone(first, near), 0, 1)
    return laid_out(blocks.reshape(-1, *array.shape), dim)


def turned_gather(arrays, axis, dims):
    turned = [jnp.moveaxis(a, dim, 0) for a, dim in zip(arrays, dims)]
    both = jnp.concatenate([t.reshape(len(t), -1) for t in turned], axis=1)
    filled, at, finished = (lax.all_gather(both, axis, axis=0, tiled=True), 0, [])
    for t, dim in zip(turned, dims):
        section = filled[:, at : at + t[0].size].reshape(-1, *t.shape[1:])
        finished.append(jnp.moveaxis(section, 0, dim))
        at += t[0].size
    return tuple(finished)


def over_copies(array, axis):
    return from_everyone(array, axis).sum(axis=0)


def one_axis_at_a_time(array, axes):
    far, near = axes
    return over_copies(over_copies(array, near), far)


def in_one(arrays, axis):
    ends = [0]
    for a in arrays:
        ends.append(ends[-1] + a.size)
    subtotal = one_axis_at_a_time(jnp.concatenate([a.ravel() for a in arrays]), axis)
    return tuple((subtotal[b:e].reshape(a.shape) for a, b, e in zip(arrays, ends, ends[1:])))


def unit_rows(matrix):
    length = jnp.sqrt(jnp.sum(matrix * matrix, axis=1, keepdims=True) + EPS_UNIT)
    return (matrix / length, length)


def unit_backward(grad_unit, unit_vec, length):
    return (grad_unit - unit_vec * jnp.sum(unit_vec * grad_unit, axis=1, keepdims=True)) / length


def per_device(images, layer_gain, in_weight, out_weight, text_embed, pair_index, logit_scale):
    multiplier = logit_scale[0]
    local_rows = images.shape[0]
    devices = lax.axis_size(DP)
    total_rows = local_rows * devices
    width = out_weight.shape[1]
    first_row = lax.axis_index(DP) * local_rows
    text_unit, text_len = unit_rows(text_embed.astype(jnp.float32))
    text_vec = text_unit.astype(jnp.bfloat16)
    all_text = whole_of(text_vec, (("dp_0", "dp_1"), ("dp_2", "dp_3")), 0)
    values = images.astype(jnp.float32)
    average = jnp.mean(values, axis=-1, keepdims=True)
    centered = values - average
    variance = jnp.mean(centered * centered, axis=-1, keepdims=True)
    normed = (centered * lax.rsqrt(variance + EPS_LAYER) * layer_gain).astype(jnp.bfloat16)
    flattened = normed.reshape(-1, normed.shape[-1])
    hidden = jax.nn.gelu(
        jnp.dot(flattened, in_weight, preferred_element_type=jnp.float32), approximate=True
    )
    pooled = jnp.mean(hidden.reshape(local_rows, images.shape[1], -1), axis=1).astype(jnp.bfloat16)
    image_emb = jnp.dot(pooled, out_weight, preferred_element_type=jnp.float32)
    image_unit, image_len = unit_rows(image_emb)
    image_vec = image_unit.astype(jnp.bfloat16)
    scores = multiplier * lax.dot_general(
        image_vec, all_text, (((1,), (1,)), ((), ())), preferred_element_type=jnp.float32
    )
    row_high = jnp.max(scores, axis=1, keepdims=True)
    row_lse = row_high[:, 0] + jnp.log(jnp.sum(jnp.exp(scores - row_high), axis=1))
    column_ids = jnp.arange(total_rows, dtype=jnp.int32)
    target = column_ids[None, :] == pair_index[:, None]
    positive = jnp.sum(jnp.where(target, scores, jnp.zeros_like(scores)), axis=1)
    all_images = whole_of(image_vec, (("dp_0", "dp_1"), ("dp_2", "dp_3")), 0)
    all_row_lse, all_pairs = turned_gather((row_lse, pair_index.astype(jnp.float32)), DP, (0, 0))
    text_scores = multiplier * lax.dot_general(
        text_vec, all_images, (((1,), (1,)), ((), ())), preferred_element_type=jnp.float32
    )
    text_high = jnp.max(text_scores, axis=1, keepdims=True)
    col_lse_own = text_high[:, 0] + jnp.log(jnp.sum(jnp.exp(text_scores - text_high), axis=1))
    own_ids = (first_row + jnp.arange(local_rows, dtype=jnp.int32)).astype(jnp.float32)
    text_target = all_pairs[None, :] == own_ids[:, None]
    text_weights = (
        jnp.exp(text_scores - all_row_lse[None, :])
        + jnp.exp(text_scores - col_lse_own[:, None])
        - 2.0 * text_target.astype(jnp.float32)
    ).astype(jnp.bfloat16)
    grad_text_unit = multiplier * jnp.dot(
        text_weights, all_images, preferred_element_type=jnp.float32
    )
    col_lse_all = whole_of(col_lse_own, (("dp_0", "dp_1"), ("dp_2", "dp_3")), 0)
    weights = (
        jnp.exp(scores - row_lse[:, None])
        + jnp.exp(scores - col_lse_all[None, :])
        - 2.0 * target.astype(jnp.float32)
    ).astype(jnp.bfloat16)
    loss_part = jnp.sum(row_lse) + jnp.sum(col_lse_own) - 2.0 * jnp.sum(positive)
    grad_image_unit = multiplier * jnp.dot(weights, all_text, preferred_element_type=jnp.float32)
    grad_image = unit_backward(grad_image_unit, image_unit, image_len)
    grad_text = unit_backward(grad_text_unit, text_unit, text_len)
    square_part = jnp.sum(grad_image * grad_image) + jnp.sum(grad_text * grad_text)
    loss_total, squares = in_one((loss_part, square_part), (("dp_0", "dp_1"), ("dp_2", "dp_3")))
    loss = loss_total / (2.0 * total_rows)
    factor = lax.rsqrt(squares / (2.0 * total_rows * width) + 1e-06)
    return (loss.reshape(1), jnp.sqrt(squares).reshape(1), grad_image * factor, grad_text * factor)


def solution(mesh):
    torus = Mesh(mesh.devices.reshape(8, 4, 4, 2), ("dp_0", "dp_1", "dp_2", "dp_3"))
    return jax.shard_map(
        per_device,
        mesh=torus,
        in_specs=(P(DP, None, None), P(), P(), P(), P(DP, None), P(DP), P()),
        out_specs=(P(), P(), P(DP, None), P(DP, None)),
        check_vma=False,
    )
```

profile of v0, /device:TPU:1, one launch (start us, length us, event | category | flops | bytes accessed | tf_op | source)
XLA Modules:
  0.0 258.0 jit_solution(7069101414245393673)
XLA Ops:
  3.2 11.9 %all-to-all-start = ((bf16[32,4,1024]{2,1,0:T(4,128)(2,1)}), bf16[32,4,1024]{2,1,0:T(4,128)(2,1)S(1)}, u32[]{:S(2)}, u32[]{:S(2)}) async-start(bf16[32,4,1024]{2,1,0:T(4,128)(2,1)} %broadcast_in_dim.20), calls=%async_computation | async-start | bytes 524288 | tf_op jit(solution)/shard_map/all_to_all | solution.py:14
  15.0 3.3 %convert_reduce_fusion = f32[4,92]{0,1:T(8,128)S(1)} fusion(bf16[4,92,4096]{2,0,1:T(4,128)(2,1)} %param.7), kind=kLoop, calls=%fused_computation.1 | loop fusion | flops 3014288 | bytes 3016128 | tf_op jit(solution)/shard_map/reduce_sum | solution.py:80
  18.3 2.1 fusion.2
  20.4 3.2 %fusion.4 = bf16[4,92,4096]{2,0,1:T(4,128)(2,1)S(1)} fusion(bf16[4,92,4096]{2,0,1:T(4,128)(2,1)S(1)} %copy-done.1, f32[4096]{0:T(1024)S(1)} %copy-done.4, f32[4,92]{0,1:T(8,128)S(1)} %add_rsqrt_fusion, f32[4,92]{0,1:T(8,128)S(1)} %broadcast_multiply_fusion), kind=kLoop, calls=%fused_computation.6 | loop fusion | flops 7536640 | bytes 6048640 | tf_op jit(solution)/shard_map/convert_element_type | solution.py:83
  23.7 3.3 %copy.27 = bf16[4,92,4096]{2,1,0:T(8,128)(2,1)} copy(bf16[4,92,4096]{2,0,1:T(4,128)(2,1)S(1)} %fusion.4) | data formatting | bytes 6029312 | tf_op jit(solution)/shard_map/convert_element_type | solution.py:83
  27.0 3.4 %reshape.128 = bf16[368,4096]{1,0:T(8,128)(2,1)} reshape(bf16[4,92,4096]{2,1,0:T(8,128)(2,1)} %copy.27) | data formatting | bytes 6029312 | tf_op jit(solution)/shard_map/reshape | solution.py:84
  30.4 9.0 %fusion.11 = f32[368,1024]{1,0:T(8,128)} fusion(bf16[368,4096]{1,0:T(8,128)(2,1)} %reshape.128, bf16[4096,1024]{1,0:T(8,128)(2,1)} %param.9), kind=kOutput, calls=%fused_computation.14 | convolution fusion | flops 3090022400 | bytes 12910592 | tf_op jit(solution)/shard_map/dot_general | solution.py:86
  39.3 2.7 %reshape.129 = f32[4,92,1024]{2,1,0:T(8,128)} reshape(f32[368,1024]{1,0:T(8,128)} %fusion.11) | data formatting | bytes 3014656 | tf_op jit(solution)/shard_map/reshape | solution.py:88
  44.3 19.8 %all_to_all.43 = bf16[32,4,1024]{2,1,0:T(4,128)(2,1)S(1)} all-to-all(bf16[32,4,1024]{2,1,0:T(4,128)(2,1)S(1)} %broadcast_in_dim.22), channel_id=1, replica_groups=mesh['dp_0'=8,'dp_1'=4,'dp_2'=4,'dp_3'=2] {'dp_0','dp_1'}, dimensions={0} | all-to-all | bytes 524288 | tf_op jit(solution)/shard_map/all_to_all | solution.py:14
  64.8 33.8 %all_to_all.44 = bf16[8,32,4,1024]{3,2,1,0:T(4,128)(2,1)} all-to-all(bf16[8,32,4,1024]{3,2,1,0:T(4,128)(2,1)S(1)} %broadcast_in_dim.21), channel_id=1, replica_groups=mesh['dp_0'=8,'dp_1'=4,'dp_2'=4,'dp_3'=2] {'dp_2','dp_3'}, dimensions={0} | all-to-all | bytes 4194304 | tf_op jit(solution)/shard_map/all_to_all | solution.py:14
  100.6 5.4 %all-to-all-start.3 = ((bf16[8,32,4,1024]{3,2,1,0:T(4,128)(2,1)}), bf16[8,32,4,1024]{3,2,1,0:T(4,128)(2,1)}, u32[]{:S(2)}, u32[]{:S(2)}) async-start(bf16[8,32,4,1024]{3,2,1,0:T(4,128)(2,1)} %broadcast_in_dim.23), calls=%async_computation.3 | async-start | bytes 4194304 | tf_op jit(solution)/shard_map/all_to_all | solution.py:14
  106.7 4.1 %copy.28 = bf16[32,8,4,1024]{3,2,1,0:T(4,128)(2,1)} copy(bf16[32,8,4,1024]{3,2,0,1:T(4,128)(2,1)} %bitcast.35) | data formatting | bytes 4194304 | tf_op jit(solution)/shard_map/transpose | solution.py:28
  110.8 4.0 %reshape_reshape.6 = bf16[1024,1024]{1,0:T(8,128)(2,1)} reshape(bf16[32,8,4,1024]{3,2,1,0:T(4,128)(2,1)} %copy.28) | data formatting | bytes 4194304 | tf_op jit(solution)/shard_map/reshape;reshape | solution.py:22
  114.8 17.6 %all-to-all-done.3 = bf16[8,32,4,1024]{3,2,1,0:T(4,128)(2,1)} async-done(((bf16[8,32,4,1024]{3,2,1,0:T(4,128)(2,1)}), bf16[8,32,4,1024]{3,2,1,0:T(4,128)(2,1)}, u32[]{:S(2)}, u32[]{:S(2)}) %all-to-all-start.3) | async-done | bytes 2097184 | tf_op jit(solution)/shard_map/all_to_all | solution.py:14
  132.4 4.1 %copy.29 = bf16[32,8,4,1024]{3,2,1,0:T(4,128)(2,1)} copy(bf16[32,8,4,1024]{3,2,0,1:T(4,128)(2,1)} %bitcast.2) | data formatting | bytes 4194304 | tf_op jit(solution)/shard_map/transpose | solution.py:28
  136.4 4.0 %reshape_reshape.7 = bf16[1024,1024]{1,0:T(8,128)(2,1)} reshape(bf16[32,8,4,1024]{3,2,1,0:T(4,128)(2,1)} %copy.29) | data formatting | bytes 4194304 | tf_op jit(solution)/shard_map/reshape;reshape | solution.py:22
  140.4 2.5 fusion.38
  145.9 3.8 %all-to-all-start.4 = ((f32[32,1,4]{2,1,0:T(1,128)}), f32[32,1,4]{2,1,0:T(1,128)S(1)}, u32[]{:S(2)}, u32[]{:S(2)}) async-start(f32[32,1,4]{2,1,0:T(1,128)} %broadcast_in_dim.25), calls=%async_computation.4 | async-start | bytes 32768 | tf_op jit(solution)/shard_map/all_to_all | solution.py:14
  149.7 63.0 %all-gather = f32[256,4,2]{1,2,0:T(2,128)S(1)} all-gather(f32[1,4,2]{1,2,0:T(2,128)S(1)} %maximum_bitcast_fusion), channel_id=1, replica_groups=mesh['dp_0'=8,'dp_1'=4,'dp_2'=4,'dp_3'=2] {'dp_0','dp_1','dp_2','dp_3'}, dimensions={0}, use_global_device_ids=true | all-gather | bytes 8224 | tf_op jit(solution)/shard_map/all_gather | solution.py:35
  212.9 2.1 multiply_reduce_fusion.1
  215.9 3.4 %all-to-all-start.5 = ((f32[8,1,128]{2,1,0:T(1,128)}), f32[8,1,128]{2,1,0:T(1,128)S(1)}, u32[]{:S(2)}, u32[]{:S(2)}) async-start(f32[8,1,128]{2,1,0:T(1,128)} %reshape.135), calls=%async_computation.5 | async-start | bytes 8192 | tf_op jit(solution)/shard_map/all_to_all | solution.py:14
  225.3 2.1 multiply_reduce_fusion.3
  229.5 7.6 %all_to_all.45 = f32[8,1,2]{2,1,0:T(1,128)S(1)} all-to-all(f32[8,1,2]{2,1,0:T(1,128)S(1)} %broadcast_in_dim.28), channel_id=1, replica_groups=mesh['dp_0'=8,'dp_1'=4,'dp_2'=4,'dp_3'=2] {'dp_2','dp_3'}, dimensions={0} | all-to-all | bytes 128 | tf_op jit(solution)/shard_map/all_to_all | solution.py:14
  237.2 14.6 %all_to_all.46 = f32[32,1,2]{2,1,0:T(1,128)S(1)} all-to-all(f32[32,1,2]{2,1,0:T(1,128)S(1)} %broadcast_in_dim.29), channel_id=1, replica_groups=mesh['dp_0'=8,'dp_1'=4,'dp_2'=4,'dp_3'=2] {'dp_0','dp_1'}, dimensions={0} | all-to-all | bytes 512 | tf_op jit(solution)/shard_map/all_to_all | solution.py:14
  (58 shorter events, 18.3 us)
Async XLA Ops:
  0.6 42.9 %copy-start = (bf16[1024,1024]{1,0:T(8,128)(2,1)S(1)}, bf16[1024,1024]{1,0:T(8,128)(2,1)}, u32[]{:S(2)}) copy-start(bf16[1024,1024]{1,0:T(8,128)(2,1)} %param.10) | copy-start | bytes 6291460
  3.2 41.0 %all-to-all-start = ((bf16[32,4,1024]{2,1,0:T(4,128)(2,1)}), bf16[32,4,1024]{2,1,0:T(4,128)(2,1)S(1)}, u32[]{:S(2)}, u32[]{:S(2)}) async-start(bf16[32,4,1024]{2,1,0:T(4,128)(2,1)} %broadcast_in_dim.20), calls=%async_computation | async-start | bytes 524288 | tf_op jit(solution)/shard_map/all_to_all | solution.py:14
  15.0 3.3 %copy-start.1 = (bf16[4,92,4096]{2,0,1:T(4,128)(2,1)S(1)}, bf16[4,92,4096]{2,0,1:T(4,128)(2,1)}, u32[]{:S(2)}) copy-start(bf16[4,92,4096]{2,0,1:T(4,128)(2,1)} %param.7) | copy-start | bytes 9043972
  18.3 2.1 copy-start.4
  100.6 6.1 %copy-start.5 = (s32[4]{0:T(128)S(1)}, s32[4]{0:T(128)}, u32[]{:S(2)}) copy-start(s32[4]{0:T(128)} %param.12) | copy-start | bytes 52
  100.6 31.8 %all-to-all-start.3 = ((bf16[8,32,4,1024]{3,2,1,0:T(4,128)(2,1)}), bf16[8,32,4,1024]{3,2,1,0:T(4,128)(2,1)}, u32[]{:S(2)}, u32[]{:S(2)}) async-start(bf16[8,32,4,1024]{3,2,1,0:T(4,128)(2,1)} %broadcast_in_dim.23), calls=%async_computation.3 | async-start | bytes 4194304 | tf_op jit(solution)/shard_map/all_to_all | solution.py:14
  140.4 2.5 copy-start.2
  142.9 70.0 %copy-start.3 = (bf16[4,1024]{1,0:T(4,128)(2,1)S(1)}, bf16[4,1024]{1,0:T(4,128)(2,1)}, u32[]{:S(2)}) copy-start(bf16[4,1024]{1,0:T(4,128)(2,1)} %param.11) | copy-start | bytes 24580
  145.9 69.2 %all-to-all-start.4 = ((f32[32,1,4]{2,1,0:T(1,128)}), f32[32,1,4]{2,1,0:T(1,128)S(1)}, u32[]{:S(2)}, u32[]{:S(2)}) async-start(f32[32,1,4]{2,1,0:T(1,128)} %broadcast_in_dim.25), calls=%async_computation.4 | async-start | bytes 32768 | tf_op jit(solution)/shard_map/all_to_all | solution.py:14
  215.9 7.9 %all-to-all-start.5 = ((f32[8,1,128]{2,1,0:T(1,128)}), f32[8,1,128]{2,1,0:T(1,128)S(1)}, u32[]{:S(2)}, u32[]{:S(2)}) async-start(f32[8,1,128]{2,1,0:T(1,128)} %reshape.135), calls=%async_computation.5 | async-start | bytes 8192 | tf_op jit(solution)/shard_map/all_to_all | solution.py:14
where the time goes:
time: 259 us; the launch traced here: 258 us
  blocking collectives  139 us (54%)
  local copies, waits for them, and re-layouts  32.1 us (12%)
  starting transfers between devices  24.5 us (9%)
  waiting for transfers between devices  19.6 us (8%)
  other arithmetic  17 us (7%)
  matrix products  17 us (7%)
  between operations  9.03 us (3%)
    all_to_all x4, blocking collectives, from_everyone(): lax.all_to_all(jnp.broadcast_to(array[None], (size, *array.shape)), axis,...  75.8 us
    all_gather x1, blocking collectives, turned_gather(): lax.all_gather(both, axis, axis=0, tiled=True)  63 us
    all_to_all x4, starting transfers between devices, from_everyone(): lax.all_to_all(jnp.broadcast_to(array[None], (size, *array.shape)), axis,...  24.5 us
    all_to_all x4, waiting for transfers between devices, from_everyone(): lax.all_to_all(jnp.broadcast_to(array[None], (size, *array.shape)), axis,...  19.6 us
    dot_general x1, matrix products, per_device(): jnp.dot(flattened, in_weight, preferred_element_type=jnp.float32)  8.96 us
    transpose x4, local copies, waits for them, and re-layouts, whole_of(): blocks = jnp.swapaxes(from_everyone(first, near), 0, 1)  8.27 us
    another operation x2, local copies, waits for them, and re-layouts, laid_out(): return jnp.moveaxis(blocks, 0, dim).reshape(lengths)  7.93 us
  transfers between devices with their start and end apart: 4, of which 2 were waited for; matrix products, arithmetic and copies ran while one was open for 16% of the time, Pallas kernels for 0%

commit v1 on v0

--- a/solution.py
+++ b/solution.py
@@ -32,7 +32,13 @@
 def turned_gather(arrays, axis, dims):
     turned = [jnp.moveaxis(a, dim, 0) for a, dim in zip(arrays, dims)]
     both = jnp.concatenate([t.reshape(len(t), -1) for t in turned], axis=1)
-    filled, at, finished = (lax.all_gather(both, axis, axis=0, tiled=True), 0, [])
+    filled, at, finished = (
+        jnp.concatenate(
+            lax.all_to_all(jnp.stack([both] * lax.axis_size(axis)), axis, 0, 0), axis=0
+        ),
+        0,
+        [],
+    )
     for t, dim in zip(turned, dims):
         section = filled[:, at : at + t[0].size].reshape(-1, *t.shape[1:])
         finished.append(jnp.moveaxis(section, 0, dim))

time: 259 us -> 222 us (0.86)
  blocking collectives: 139 us -> 73.3 us
  waiting for transfers between devices: 19.6 us -> 39.9 us
  starting transfers between devices: 24.5 us -> 32.3 us
    all_gather x1 -> x0, blocking collectives: 63 us -> none  [turned_gather(): lax.all_gather(both, axis, axis=0, tiled=True)]
    all_to_all x0 -> x1, waiting for transfers between devices: none -> 11.1 us  [turned_gather(): lax.all_to_all(jnp.stack([both] * lax.axis_size(axis)), axis, 0, 0)]
    all_to_all x4, waiting for transfers between devices: 19.6 us -> 28.8 us  [from_everyone(): lax.all_to_all(jnp.broadcast_to(array[None], (size, *array.shape)), axis,...]
    all_to_all x0 -> x1, starting transfers between devices: none -> 5.7 us  [turned_gather(): lax.all_to_all(jnp.stack([both] * lax.axis_size(axis)), axis, 0, 0)]
  transfers between devices with their start and end apart: 4 -> 5, of which waited for: 2 -> 4; matrix products, arithmetic and copies ran while one was open for 16% -> 19% of each run, Pallas kernels for 0% -> 0%
where the time goes in v1:
time: 222 us; the launch traced here: 221 us
  blocking collectives  73.3 us (33%)
  waiting for transfers between devices  39.9 us (18%)
  local copies, waits for them, and re-layouts  32.9 us (15%)
  starting transfers between devices  32.3 us (15%)
  other arithmetic  17 us (8%)
  matrix products  17 us (8%)
  between operations  9.05 us (4%)
    all_to_all x4, blocking collectives, from_everyone(): lax.all_to_all(jnp.broadcast_to(array[None], (size, *array.shape)), axis,...  73.3 us
    all_to_all x4, waiting for transfers between devices, from_everyone(): lax.all_to_all(jnp.broadcast_to(array[None], (size, *array.shape)), axis,...  28.8 us
    all_to_all x4, starting transfers between devices, from_everyone(): lax.all_to_all(jnp.broadcast_to(array[None], (size, *array.shape)), axis,...  26.6 us
    all_to_all x1, waiting for transfers between devices, turned_gather(): lax.all_to_all(jnp.stack([both] * lax.axis_size(axis)), axis, 0, 0)  11.1 us
    dot_general x1, matrix products, per_device(): jnp.dot(flattened, in_weight, preferred_element_type=jnp.float32)  8.96 us
    transpose x4, local copies, waits for them, and re-layouts, whole_of(): blocks = jnp.swapaxes(from_everyone(first, near), 0, 1)  8.27 us
    another operation x2, local copies, waits for them, and re-layouts, laid_out(): return jnp.moveaxis(blocks, 0, dim).reshape(lengths)  7.93 us
    all_to_all x1, starting transfers between devices, turned_gather(): lax.all_to_all(jnp.stack([both] * lax.axis_size(axis)), axis, 0, 0)  5.7 us
  transfers between devices with their start and end apart: 5, of which 4 were waited for; matrix products, arithmetic and copies ran while one was open for 19% of the time, Pallas kernels for 0%

profile of v1, /device:TPU:1, one launch (start us, length us, event | category | flops | bytes accessed | tf_op | source)
XLA Modules:
  0.0 221.3 jit_solution(17670499168763801336)
XLA Ops:
  3.2 11.9 %all-to-all-start = ((bf16[32,4,1024]{2,1,0:T(4,128)(2,1)}), bf16[32,4,1024]{2,1,0:T(4,128)(2,1)S(1)}, u32[]{:S(2)}, u32[]{:S(2)}) async-start(bf16[32,4,1024]{2,1,0:T(4,128)(2,1)} %broadcast_in_dim.20), calls=%async_computation | async-start | bytes 524288 | tf_op jit(solution)/shard_map/all_to_all | solution.py:14
  15.0 3.3 %convert_reduce_fusion = f32[4,92]{0,1:T(8,128)S(1)} fusion(bf16[4,92,4096]{2,0,1:T(4,128)(2,1)} %param.7), kind=kLoop, calls=%fused_computation.1 | loop fusion | flops 3014288 | bytes 3016128 | tf_op jit(solution)/shard_map/reduce_sum | solution.py:86
  20.4 3.2 %fusion.4 = bf16[4,92,4096]{2,0,1:T(4,128)(2,1)S(1)} fusion(bf16[4,92,4096]{2,0,1:T(4,128)(2,1)S(1)} %copy-done.1, f32[4096]{0:T(1024)S(1)} %copy-done.4, f32[4,92]{0,1:T(8,128)S(1)} %add_rsqrt_fusion, f32[4,92]{0,1:T(8,128)S(1)} %broadcast_multiply_fusion), kind=kLoop, calls=%fused_computation.6 | loop fusion | flops 7536640 | bytes 6048640 | tf_op jit(solution)/shard_map/convert_element_type | solution.py:89
  23.7 3.3 %copy.29 = bf16[4,92,4096]{2,1,0:T(8,128)(2,1)} copy(bf16[4,92,4096]{2,0,1:T(4,128)(2,1)S(1)} %fusion.4) | data formatting | bytes 6029312 | tf_op jit(solution)/shard_map/convert_element_type | solution.py:89
  27.0 3.4 %reshape.133 = bf16[368,4096]{1,0:T(8,128)(2,1)} reshape(bf16[4,92,4096]{2,1,0:T(8,128)(2,1)} %copy.29) | data formatting | bytes 6029312 | tf_op jit(solution)/shard_map/reshape | solution.py:90
  30.4 9.0 %fusion.11 = f32[368,1024]{1,0:T(8,128)} fusion(bf16[368,4096]{1,0:T(8,128)(2,1)} %reshape.133, bf16[4096,1024]{1,0:T(8,128)(2,1)} %param.9), kind=kOutput, calls=%fused_computation.14 | convolution fusion | flops 3090022400 | bytes 12910592 | tf_op jit(solution)/shard_map/dot_general | solution.py:92
  39.3 2.7 %reshape.134 = f32[4,92,1024]{2,1,0:T(8,128)} reshape(f32[368,1024]{1,0:T(8,128)} %fusion.11) | data formatting | bytes 3014656 | tf_op jit(solution)/shard_map/reshape | solution.py:94
  44.3 19.8 %all_to_all.48 = bf16[32,4,1024]{2,1,0:T(4,128)(2,1)S(1)} all-to-all(bf16[32,4,1024]{2,1,0:T(4,128)(2,1)S(1)} %broadcast_in_dim.22), channel_id=1, replica_groups=mesh['dp_0'=8,'dp_1'=4,'dp_2'=4,'dp_3'=2] {'dp_0','dp_1'}, dimensions={0} | all-to-all | bytes 524288 | tf_op jit(solution)/shard_map/all_to_all | solution.py:14
  64.8 33.8 %all_to_all.49 = bf16[8,32,4,1024]{3,2,1,0:T(4,128)(2,1)} all-to-all(bf16[8,32,4,1024]{3,2,1,0:T(4,128)(2,1)S(1)} %broadcast_in_dim.21), channel_id=1, replica_groups=mesh['dp_0'=8,'dp_1'=4,'dp_2'=4,'dp_3'=2] {'dp_2','dp_3'}, dimensions={0} | all-to-all | bytes 4194304 | tf_op jit(solution)/shard_map/all_to_all | solution.py:14
  100.6 5.4 %all-to-all-start.3 = ((bf16[8,32,4,1024]{3,2,1,0:T(4,128)(2,1)}), bf16[8,32,4,1024]{3,2,1,0:T(4,128)(2,1)}, u32[]{:S(2)}, u32[]{:S(2)}) async-start(bf16[8,32,4,1024]{3,2,1,0:T(4,128)(2,1)} %broadcast_in_dim.23), calls=%async_computation.3 | async-start | bytes 4194304 | tf_op jit(solution)/shard_map/all_to_all | solution.py:14
  106.7 4.1 %copy.30 = bf16[32,8,4,1024]{3,2,1,0:T(4,128)(2,1)} copy(bf16[32,8,4,1024]{3,2,0,1:T(4,128)(2,1)} %bitcast.33) | data formatting | bytes 4194304 | tf_op jit(solution)/shard_map/transpose | solution.py:28
  110.8 4.0 %reshape_reshape.6 = bf16[1024,1024]{1,0:T(8,128)(2,1)} reshape(bf16[32,8,4,1024]{3,2,1,0:T(4,128)(2,1)} %copy.30) | data formatting | bytes 4194304 | tf_op jit(solution)/shard_map/reshape;reshape | solution.py:22
  114.8 17.6 %all-to-all-done.3 = bf16[8,32,4,1024]{3,2,1,0:T(4,128)(2,1)} async-done(((bf16[8,32,4,1024]{3,2,1,0:T(4,128)(2,1)}), bf16[8,32,4,1024]{3,2,1,0:T(4,128)(2,1)}, u32[]{:S(2)}, u32[]{:S(2)}) %all-to-all-start.3) | async-done | bytes 2097184 | tf_op jit(solution)/shard_map/all_to_all | solution.py:14
  132.4 4.1 %copy.31 = bf16[32,8,4,1024]{3,2,1,0:T(4,128)(2,1)} copy(bf16[32,8,4,1024]{3,2,0,1:T(4,128)(2,1)} %bitcast.2) | data formatting | bytes 4194304 | tf_op jit(solution)/shard_map/transpose | solution.py:28
  136.4 4.0 %reshape_reshape.7 = bf16[1024,1024]{1,0:T(8,128)(2,1)} reshape(bf16[32,8,4,1024]{3,2,1,0:T(4,128)(2,1)} %copy.31) | data formatting | bytes 4194304 | tf_op jit(solution)/shard_map/reshape;reshape | solution.py:22
  140.4 2.5 %fusion.38 = (f32[4]{0:T(128)S(1)}, f32[4,1024]{1,0:T(4,128)S(1)}) fusion(bf16[4,1024]{1,0:T(4,128)(2,1)S(1)} %get-tuple-element.14, bf16[1024,1024]{1,0:T(8,128)(2,1)} %reshape_reshape.6, f32[]{:T(128)} %bitcast.29), kind=kOutput, calls=%fused_computation.74 | convolution fusion | flops 8396796 | bytes 2121748 | tf_op jit(solution)/shard_map/dot_general | solution.py:98
  145.9 3.8 %all-to-all-start.4 = ((f32[32,1,4]{2,1,0:T(1,128)}), f32[32,1,4]{2,1,0:T(1,128)S(1)}, u32[]{:S(2)}, u32[]{:S(2)}) async-start(f32[32,1,4]{2,1,0:T(1,128)} %broadcast_in_dim.25), calls=%async_computation.4 | async-start | bytes 32768 | tf_op jit(solution)/shard_map/all_to_all | solution.py:14
  149.7 8.5 %all-to-all-done.4 = f32[32,1,4]{2,1,0:T(1,128)S(1)} async-done(((f32[32,1,4]{2,1,0:T(1,128)}), f32[32,1,4]{2,1,0:T(1,128)S(1)}, u32[]{:S(2)}, u32[]{:S(2)}) %all-to-all-start.4) | async-done | bytes 544 | tf_op jit(solution)/shard_map/all_to_all | solution.py:14
  159.0 5.5 %all-to-all-start.5 = ((f32[8,1,128]{2,1,0:T(1,128)}), f32[8,1,128]{2,1,0:T(1,128)S(1)}, u32[]{:S(2)}, u32[]{:S(2)}) async-start(f32[8,1,128]{2,1,0:T(1,128)} %reshape.139), calls=%async_computation.5 | async-start | bytes 8192 | tf_op jit(solution)/shard_map/all_to_all | solution.py:14
  166.4 2.6 %all-to-all-done.5 = f32[8,1,128]{2,1,0:T(1,128)S(1)} async-done(((f32[8,1,128]{2,1,0:T(1,128)}), f32[8,1,128]{2,1,0:T(1,128)S(1)}, u32[]{:S(2)}, u32[]{:S(2)}) %all-to-all-start.5) | async-done | bytes 4128 | tf_op jit(solution)/shard_map/all_to_all | solution.py:14
  169.8 5.7 %all-to-all-start.6 = ((f32[256,4,2]{1,2,0:T(2,128)}), f32[256,4,2]{1,2,0:T(2,128)S(1)}, u32[]{:S(2)}, u32[]{:S(2)}) async-start(f32[256,4,2]{1,2,0:T(2,128)} %stack.2), calls=%async_computation.6 | async-start | bytes 524288 | tf_op jit(solution)/shard_map/all_to_all | solution.py:37
  179.9 11.1 %all-to-all-done.6 = f32[256,4,2]{1,2,0:T(2,128)S(1)} async-done(((f32[256,4,2]{1,2,0:T(2,128)}), f32[256,4,2]{1,2,0:T(2,128)S(1)}, u32[]{:S(2)}, u32[]{:S(2)}) %all-to-all-start.6) | async-done | bytes 8224 | tf_op jit(solution)/shard_map/all_to_all | solution.py:37
  195.4 8.0 %all_to_all.50 = f32[8,1,2]{2,1,0:T(1,128)S(1)} all-to-all(f32[8,1,2]{2,1,0:T(1,128)S(1)} %broadcast_in_dim.28), channel_id=1, replica_groups=mesh['dp_0'=8,'dp_1'=4,'dp_2'=4,'dp_3'=2] {'dp_2','dp_3'}, dimensions={0} | all-to-all | bytes 128 | tf_op jit(solution)/shard_map/all_to_all | solution.py:14
  203.5 11.6 %all_to_all.51 = f32[32,1,2]{2,1,0:T(1,128)S(1)} all-to-all(f32[32,1,2]{2,1,0:T(1,128)S(1)} %broadcast_in_dim.29), channel_id=1, replica_groups=mesh['dp_0'=8,'dp_1'=4,'dp_2'=4,'dp_3'=2] {'dp_0','dp_1'}, dimensions={0} | all-to-all | bytes 512 | tf_op jit(solution)/shard_map/all_to_all | solution.py:14
  (60 shorter events, 23.5 us)
Async XLA Ops:
  0.6 42.9 %copy-start = (bf16[1024,1024]{1,0:T(8,128)(2,1)S(1)}, bf16[1024,1024]{1,0:T(8,128)(2,1)}, u32[]{:S(2)}) copy-start(bf16[1024,1024]{1,0:T(8,128)(2,1)} %param.10) | copy-start | bytes 6291460
  3.2 41.0 %all-to-all-start = ((bf16[32,4,1024]{2,1,0:T(4,128)(2,1)}), bf16[32,4,1024]{2,1,0:T(4,128)(2,1)S(1)}, u32[]{:S(2)}, u32[]{:S(2)}) async-start(bf16[32,4,1024]{2,1,0:T(4,128)(2,1)} %broadcast_in_dim.20), calls=%async_computation | async-start | bytes 524288 | tf_op jit(solution)/shard_map/all_to_all | solution.py:14
  15.0 3.3 %copy-start.1 = (bf16[4,92,4096]{2,0,1:T(4,128)(2,1)S(1)}, bf16[4,92,4096]{2,0,1:T(4,128)(2,1)}, u32[]{:S(2)}) copy-start(bf16[4,92,4096]{2,0,1:T(4,128)(2,1)} %param.7) | copy-start | bytes 9043972
  18.3 2.1 copy-start.4
  100.6 6.1 %copy-start.5 = (s32[4]{0:T(128)S(1)}, s32[4]{0:T(128)}, u32[]{:S(2)}) copy-start(s32[4]{0:T(128)} %param.12) | copy-start | bytes 52
  100.6 31.8 %all-to-all-start.3 = ((bf16[8,32,4,1024]{3,2,1,0:T(4,128)(2,1)}), bf16[8,32,4,1024]{3,2,1,0:T(4,128)(2,1)}, u32[]{:S(2)}, u32[]{:S(2)}) async-start(bf16[8,32,4,1024]{3,2,1,0:T(4,128)(2,1)} %broadcast_in_dim.23), calls=%async_computation.3 | async-start | bytes 4194304 | tf_op jit(solution)/shard_map/all_to_all | solution.py:14
  140.4 2.5 %copy-start.2 = (bf16[1024,1024]{1,0:T(8,128)(2,1)S(1)}, bf16[1024,1024]{1,0:T(8,128)(2,1)}, u32[]{:S(2)}) copy-start(bf16[1024,1024]{1,0:T(8,128)(2,1)} %reshape_reshape.7) | copy-start | bytes 6291460
  145.9 12.4 %all-to-all-start.4 = ((f32[32,1,4]{2,1,0:T(1,128)}), f32[32,1,4]{2,1,0:T(1,128)S(1)}, u32[]{:S(2)}, u32[]{:S(2)}) async-start(f32[32,1,4]{2,1,0:T(1,128)} %broadcast_in_dim.25), calls=%async_computation.4 | async-start | bytes 32768 | tf_op jit(solution)/shard_map/all_to_all | solution.py:14
  159.0 32.2 %copy-start.3 = (bf16[4,1024]{1,0:T(4,128)(2,1)S(1)}, bf16[4,1024]{1,0:T(4,128)(2,1)}, u32[]{:S(2)}) copy-start(bf16[4,1024]{1,0:T(4,128)(2,1)} %param.11) | copy-start | bytes 24580
  159.0 10.0 %all-to-all-start.5 = ((f32[8,1,128]{2,1,0:T(1,128)}), f32[8,1,128]{2,1,0:T(1,128)S(1)}, u32[]{:S(2)}, u32[]{:S(2)}) async-start(f32[8,1,128]{2,1,0:T(1,128)} %reshape.139), calls=%async_computation.5 | async-start | bytes 8192 | tf_op jit(solution)/shard_map/all_to_all | solution.py:14
  169.8 21.1 %all-to-all-start.6 = ((f32[256,4,2]{1,2,0:T(2,128)}), f32[256,4,2]{1,2,0:T(2,128)S(1)}, u32[]{:S(2)}, u32[]{:S(2)}) async-start(f32[256,4,2]{1,2,0:T(2,128)} %stack.2), calls=%async_computation.6 | async-start | bytes 524288 | tf_op jit(solution)/shard_map/all_to_all | solution.py:37
